TPU v7x, 512 devices: a whole 4x8x8 slice. The times are simulated.
512 devices in a mesh: row: 8 (over y), col: 32 (over z, x), rep: 2 (over core).
Axes of the slice: x: 4, y: 8, z: 8, core: 2. Of those that a mesh axis runs over, the one named last changes fastest.
Arguments:
- gain: float32 [768, 8, 128, 128], P(('row', 'col'), 'rep'), as said below
- coupled_columns: int32 [768, 8], P(('row', 'col')), may hold values from 0 to 767, as said below
- solution: float32 [98304, 512], P(('row', 'col')), may hold values from -6 to 6
- residual: float32 [98304, 512], P(('row', 'col')), may hold values from -6 to 6
- direction: float32 [98304, 512], P(('row', 'col')), may hold values from -6 to 6
Outputs:
- solution_next: float32 [98304, 512], P(('row', 'col'))
- residual_next: float32 [98304, 512], P(('row', 'col'))
- direction_next: float32 [98304, 512], P(('row', 'col'))
Inputs may be any that keep to these rules, and one draw needn't show every extreme that they name: `coupled_columns`: each block row i names first its coupled block columns in ascending order (always i - 1, i, i + 1 where inside 0 to 767, some of i - 3, i - 2, i + 2, i + 3, the coupling being symmetric), at most 7 of them, and then fills the remaining slots with i itself; every named column is within 3 of i. The gain matrix assembled from its blocks is symmetric; padding slots hold zero blocks; each diagonal entry exceeds the sum of the absolute values of the other entries of its row by exactly 1.
All inputs are finite; a program needn't handle non-finite values.
Results may differ from a plain program's by a relative error of at most 0.000061.
Values sent between devices are 32-bit elements; how exact they have to be, the bound alone decides.
No kernel may reach another device: no remote copies, remote signals or barrier semaphores. Data moves between devices by JAX's collectives and lax.ppermute only.
A program may use at most 64 MiB of HBM per device.

v0:
```python
import functools

import jax
import jax.numpy as jnp
from jax import lax
from jax.sharding import Mesh
from jax.sharding import PartitionSpec as P

BLK = 128
ROW_COL = ("row", "col_0", "col_1")


reach_blocks = 3


def extended_2(block, sides, width):
    for axis, dim in sides:
        count = lax.axis_size(axis)
        forward = [(i, i + 1) for i in range(count - 1)]
        backward = [(target, source) for source, target in forward]
        low = lax.ppermute(
            lax.slice_in_dim(block, block.shape[dim] - width, None, axis=dim), axis, forward
        )
        high = lax.ppermute(lax.slice_in_dim(block, 0, width, axis=dim), axis, backward)
        block = jnp.concatenate([low, block, high], axis=dim)
    return block


def copy_for_each(x, axis):
    count = lax.axis_size(axis)
    return lax.all_to_all(jnp.broadcast_to(x[None], (count, *x.shape)), axis, 0, 0, tiled=True)


def laid_out(pieces, dim):
    shape = list(pieces.shape[1:])
    shape[dim] *= pieces.shape[0]
    return jnp.moveaxis(pieces, 0, dim).reshape(shape)


def gather_directly(x, axis, dim):
    pieces = copy_for_each(x, axis)
    return laid_out(pieces, dim)


def over_axes(x, axes):
    return functools.reduce(lax.psum, axes, x)


def per_device(gain, coupled_columns, solution, residual, direction):
    row_blocks = coupled_columns.shape[0]
    snapshots = direction.shape[1]
    first_block = lax.axis_index(ROW_COL) * row_blocks
    extended = extended_2(direction, ((ROW_COL, 0),), reach_blocks * BLK)
    segments = extended.reshape(row_blocks + 2 * reach_blocks, BLK, snapshots)
    all_blocks = gather_directly(gain, "rep", 1)
    local_index = coupled_columns - first_block + reach_blocks
    picked = segments[local_index]
    product = jnp.einsum(
        "rkab,rkbs->ras",
        all_blocks,
        picked,
        precision=lax.Precision.HIGHEST,
        preferred_element_type=jnp.float32,
    )
    image = product.reshape(row_blocks * BLK, snapshots)
    norm_old, curvature, crossing, image_square = (
        over_axes(jnp.sum(residual * residual, axis=0), ROW_COL),
        over_axes(jnp.sum(direction * image, axis=0), ROW_COL),
        over_axes(jnp.sum(residual * image, axis=0), ROW_COL),
        over_axes(jnp.sum(image * image, axis=0), ROW_COL),
    )
    step_size = norm_old / curvature
    solution_next = solution + step_size * direction
    residual_next = residual - step_size * image
    norm_new = norm_old - 2.0 * step_size * crossing + step_size * step_size * image_square
    direction_next = residual_next + norm_new / norm_old * direction
    return (solution_next, residual_next, direction_next)


def solution(mesh):
    finer = Mesh(
        mesh.devices.reshape(mesh.shape["row"], 8, 4, mesh.shape["rep"]),
        ("row", "col_0", "col_1", "rep"),
    )
    return jax.shard_map(
        per_device,
        mesh=finer,
        in_specs=(
            P(ROW_COL, "rep", None, None),
            P(ROW_COL, None),
            P(ROW_COL, None),
            P(ROW_COL, None),
            P(ROW_COL, None),
        ),
        out_specs=(P(ROW_COL, None), P(ROW_COL, None), P(ROW_COL, None)),
        check_vma=False,
    )
```

profile of v0, /device:TPU:8, one launch (start us, length us, event | category | flops | bytes accessed | tf_op | source)
XLA Modules:
  0.0 92.6 jit_solution(12023885535477547986)
XLA Ops:
  0.6 0.0 copy-start.4
  0.6 3.4 %collective-permute-start = (f32[384,512]{1,0:T(8,128)}, f32[384,512]{1,0:T(8,128)S(1)}, u32[]{:S(2)}, u32[]{:S(2)}) collective-permute-start(f32[384,512]{1,0:T(8,128)} %param.9), channel_id=1, source_target_pairs={{0,2},{2,4},{4,6},{6,8},{8,10},{10,12},{12,14},{14,16},{16,18},{18... | collective-permute-start | bytes 2359304 | tf_op jit(solution)/shard_map/ppermute | solution.py:21
  4.0 11.6 %collective-permute-start.1 = (f32[384,512]{1,0:T(8,128)}, f32[384,512]{1,0:T(8,128)}, u32[]{:S(2)}, u32[]{:S(2)}) collective-permute-start(f32[384,512]{1,0:T(8,128)} %param.9), channel_id=1, source_target_pairs={{2,0},{4,2},{6,4},{8,6},{10,8},{12,10},{14,12},{16,14},{18,16},{20... | collective-permute-start | bytes 2359304 | tf_op jit(solution)/shard_map/ppermute | solution.py:24
  15.6 2.5 %broadcast_in_dim.5 = f32[2,3,4,128,128]{4,3,2,1,0:T(8,128)} broadcast(f32[3,4,128,128]{3,2,1,0:T(8,128)} %param.5), dimensions={1,2,3,4} | broadcast | bytes 2359296 | tf_op jit(solution)/shard_map/broadcast_in_dim | solution.py:31
  18.1 3.7 %all-to-all-start = ((f32[2,3,4,128,128]{4,3,2,1,0:T(8,128)}), f32[2,3,4,128,128]{4,3,2,1,0:T(8,128)S(1)}, u32[]{:S(2)}, u32[]{:S(2)}) async-start(f32[2,3,4,128,128]{4,3,2,1,0:T(8,128)} %broadcast_in_dim.5), calls=%async_computation | async-start | bytes 3145728 | tf_op jit(solution)/shard_map/all_to_all | solution.py:31
  21.7 0.0 copy-start
  21.8 0.0 copy-done.4
  21.8 0.1 reshape.23
  21.9 2.4 %all-to-all-done = f32[2,3,4,128,128]{4,3,2,1,0:T(8,128)S(1)} async-done(((f32[2,3,4,128,128]{4,3,2,1,0:T(8,128)}), f32[2,3,4,128,128]{4,3,2,1,0:T(8,128)S(1)}, u32[]{:S(2)}, u32[]{:S(2)}) %all-to-all-start) | async-done | bytes 1572896 | tf_op jit(solution)/shard_map/all_to_all | solution.py:31
  24.2 1.2 %copy.8 = f32[3,2,4,128,128]{4,3,2,1,0:T(8,128)} copy(f32[3,2,4,128,128]{4,3,2,0,1:T(8,128)S(1)} %bitcast.27) | data formatting | bytes 3145728 | tf_op jit(solution)/shard_map/transpose | solution.py:37
  25.5 5.9 %collective-permute-done = f32[384,512]{1,0:T(8,128)S(1)} collective-permute-done((f32[384,512]{1,0:T(8,128)}, f32[384,512]{1,0:T(8,128)S(1)}, u32[]{:S(2)}, u32[]{:S(2)}) %collective-permute-start) | collective-permute-done | bytes 786464 | tf_op jit(solution)/shard_map/ppermute | solution.py:21
  31.4 0.9 copy-done.3
  32.3 0.4 collective-permute-done.1
  32.7 0.0 copy-done
  32.7 1.6 %pad_maximum_fusion = f32[1152,512]{1,0:T(8,128)S(1)} fusion(f32[384,512]{1,0:T(8,128)} %collective-permute-done.1, f32[384,512]{1,0:T(8,128)S(1)} %copy-done, f32[384,512]{1,0:T(8,128)} %copy-done.3), kind=kLoop, calls=%fused_computation.1 | loop fusion | flops 1179648 | bytes 4718592 | tf_op jit(solution)/shard_map/concatenate | solution.py:25
  34.3 3.6 %gather_fusion = f32[24,128,512]{2,1,0:T(8,128)} fusion(f32[9,128,512]{2,1,0:T(8,128)S(1)} %bitcast.25, s32[1024]{0:T(1024)S(1)} %pad_clamp_fusion), kind=kCustom, calls=%fused_computation | custom fusion | bytes 12583008 | tf_op jit(solution)/shard_map/gather | solution.py:57
  37.9 6.7 %fusion.3 = (f32[512]{0:T(512)S(1)}, f32[3,512,128,1]{1,2,3,0:T(8,128)S(1)}) fusion(f32[3,8,128,512]{3,2,1,0:T(8,128)} %bitcast.26, f32[3,8,128,128]{3,2,1,0:T(8,128)} %bitcast.28), kind=kOutput, calls=%fused_computation.9 | convolution fusion | flops 2416311808 | bytes 8652800 | tf_op jit(solution)/shard_map/rkab,rkbs->ras/dot_general | solution.py:58
  44.6 0.0 copy-start.2
  44.6 0.0 copy-done.1
  44.6 0.3 fusion.2
  44.9 17.3 %all-reduce.1 = (f32[512]{0:T(512)S(1)}, f32[512]{0:T(512)S(1)}, f32[512]{0:T(512)S(1)}, f32[512]{0:T(512)S(1)}) all-reduce(f32[512]{0:T(512)S(1)} %get-tuple-element.5, f32[512]{0:T(512)S(1)} %get-tuple-element.4, f32[512]{0:T(512)S(1)} %get-tuple-element.23, ...), channel_id=1, replica_groups=mesh['row'=8,'col_0'=8,'col_1'=4,'rep'=2] {'row'}, use_global_device_ids=true, to_apply=%region_1.0 | all-reduce | flops 2048 | bytes 16384 | tf_op jit(solution)/shard_map/psum | solution.py:46
  62.2 15.2 %all-reduce = (f32[512]{0:T(512)S(1)}, f32[512]{0:T(512)S(1)}, f32[512]{0:T(512)S(1)}, f32[512]{0:T(512)S(1)}) all-reduce(f32[512]{0:T(512)S(1)} %get-tuple-element.10, f32[512]{0:T(512)S(1)} %get-tuple-element.11, f32[512]{0:T(512)S(1)} %get-tuple-element.12, ...), channel_id=1, replica_groups=mesh['row'=8,'col_0'=8,'col_1'=4,'rep'=2] {'col_0'}, use_global_device_ids=true, to_apply=%region_2.0 | all-reduce | flops 2048 | bytes 16384 | tf_op jit(solution)/shard_map/psum | solution.py:46
  77.5 13.4 %all-reduce.2 = (f32[512]{0:T(512)S(1)}, f32[512]{0:T(512)S(1)}, f32[512]{0:T(512)S(1)}, f32[512]{0:T(512)S(1)}) all-reduce(f32[512]{0:T(512)S(1)} %get-tuple-element.6, f32[512]{0:T(512)S(1)} %get-tuple-element.7, f32[512]{0:T(512)S(1)} %get-tuple-element.8, ...), channel_id=1, replica_groups=mesh['row'=8,'col_0'=8,'col_1'=4,'rep'=2] {'col_1'}, use_global_device_ids=true, to_apply=%region_3.0 | all-reduce | flops 2048 | bytes 16384 | tf_op jit(solution)/shard_map/psum | solution.py:46
  91.0 1.7 %multiply_add_fusion = (f32[384,512]{1,0:T(8,128)}, f32[384,512]{1,0:T(8,128)}, f32[384,512]{1,0:T(8,128)}) fusion(f32[384,512]{1,0:T(8,128)S(1)} %copy-done, f32[512]{0:T(512)S(1)} %get-tuple-element.20, f32[384,512]{1,0:T(8,128)S(1)} %copy-done.1, f32[3,512,128,1]{1,2,3,0:T(8,128)S(1)} %get-tuple-element.24, f32[512]{0:T(512)S(1)} %get-tuple-element.21, ...), kind=kLoop, calls=%fused_computation.10 | loop fusion | flops 1179648 | bytes 5509120 | tf_op jit(solution)/shard_map/add | solution.py:76
  (6 shorter events, 0.0 us)
Async XLA Ops:
  0.6 21.1 %copy-start.4 = (s32[3,8]{1,0:T(4,128)S(1)}, s32[3,8]{1,0:T(4,128)}, u32[]{:S(2)}) copy-start(s32[3,8]{1,0:T(4,128)} %param.6) | copy-start | bytes 292
  0.6 30.8 %collective-permute-start = (f32[384,512]{1,0:T(8,128)}, f32[384,512]{1,0:T(8,128)S(1)}, u32[]{:S(2)}, u32[]{:S(2)}) collective-permute-start(f32[384,512]{1,0:T(8,128)} %param.9), channel_id=1, source_target_pairs={{0,2},{2,4},{4,6},{6,8},{8,10},{10,12},{12,14},{14,16},{16,18},{18... | collective-permute-start | bytes 2359304 | tf_op jit(solution)/shard_map/ppermute | solution.py:21
  4.0 28.7 %collective-permute-start.1 = (f32[384,512]{1,0:T(8,128)}, f32[384,512]{1,0:T(8,128)}, u32[]{:S(2)}, u32[]{:S(2)}) collective-permute-start(f32[384,512]{1,0:T(8,128)} %param.9), channel_id=1, source_target_pairs={{2,0},{4,2},{6,4},{8,6},{10,8},{12,10},{14,12},{16,14},{18,16},{20... | collective-permute-start | bytes 2359304 | tf_op jit(solution)/shard_map/ppermute | solution.py:24
  18.1 6.2 %all-to-all-start = ((f32[2,3,4,128,128]{4,3,2,1,0:T(8,128)}), f32[2,3,4,128,128]{4,3,2,1,0:T(8,128)S(1)}, u32[]{:S(2)}, u32[]{:S(2)}) async-start(f32[2,3,4,128,128]{4,3,2,1,0:T(8,128)} %broadcast_in_dim.5), calls=%async_computation | async-start | bytes 3145728 | tf_op jit(solution)/shard_map/all_to_all | solution.py:31
  21.7 11.0 %copy-start = (f32[384,512]{1,0:T(8,128)S(1)}, f32[384,512]{1,0:T(8,128)}, u32[]{:S(2)}) copy-start(f32[384,512]{1,0:T(8,128)} %param.9) | copy-start | bytes 2359300
  31.4 0.9 copy-start.3
  37.9 6.7 %copy-start.1 = (f32[384,512]{1,0:T(8,128)S(1)}, f32[384,512]{1,0:T(8,128)}, u32[]{:S(2)}) copy-start(f32[384,512]{1,0:T(8,128)} %param.8) | copy-start | bytes 2359300
  44.6 46.3 %copy-start.2 = (f32[384,512]{1,0:T(8,128)S(1)}, f32[384,512]{1,0:T(8,128)}, u32[]{:S(2)}) copy-start(f32[384,512]{1,0:T(8,128)} %param.7) | copy-start | bytes 2359300
where the time goes:
time: 93 us; the launch traced here: 92.6 us
  blocking collectives  46 us (49%)
  starting transfers between devices  18.6 us (20%)
  waiting for transfers between devices  8.69 us (9%)
  local copies, waits for them, and re-layouts  8.3 us (9%)
  matrix products  6.7 us (7%)
  other arithmetic  3.58 us (4%)
    psum x3, blocking collectives, over_axes(): return functools.reduce(lax.psum, axes, x)  46 us
    ppermute x1, starting transfers between devices, extended_2(): lax.ppermute(lax.slice_in_dim(block, 0, width, axis=dim), axis, backward)  11.6 us
    dot_general x1, matrix products, per_device(): jnp.einsum('rkab,rkbs->ras', all_blocks, picked, precision=lax.Precision....  6.7 us
    ppermute x1, waiting for transfers between devices, extended_2(): lax.ppermute(lax.slice_in_dim(block, block.shape[dim] - width, None, axis...  5.93 us
    all_to_all x1, starting transfers between devices, copy_for_each(): lax.all_to_all(jnp.broadcast_to(x[None], (count, *x.shape)), axis, 0, 0,...  3.67 us
    gather x1, local copies, waits for them, and re-layouts, per_device(): picked = segments[local_index]  3.61 us
    ppermute x1, starting transfers between devices, extended_2(): lax.ppermute(lax.slice_in_dim(block, block.shape[dim] - width, None, axis...  3.4 us
    broadcast_in_dim x1, local copies, waits for them, and re-layouts, copy_for_each(): jnp.broadcast_to(x[None], (count, *x.shape))  2.46 us
  transfers between devices with their start and end apart: 3, of which 3 were waited for; matrix products, arithmetic and copies ran while one was open for 4% of the time, Pallas kernels for 0%

commit v1 on v0

v1 whole, which is shorter than its diff:
```python
import jax
import jax.numpy as jnp
from jax import lax
from jax.sharding import Mesh
from jax.sharding import PartitionSpec as P

BLK = 128
REACH = 3
ROW_COL = ("row", "col_0", "col_1")
ALL = ("row", "col_0", "col_1", "rep")


def halo_pairs(groups, step):
    pairs = []
    for p in range(groups):
        for rep, to in ((0, p + step), (1, p - step)):
            if 0 <= to < groups:
                pairs.append((2 * p + rep, 2 * to + rep))
    return pairs


def from_all(x, axes, count):
    return lax.all_to_all(jnp.broadcast_to(x[None], (count, *x.shape)), axes, 0, 0, tiled=True)


def per_device(gain, coupled_columns, solution, residual, direction):
    rows = coupled_columns.shape[0]
    snapshots = direction.shape[1]
    half = snapshots // 2
    rep = lax.axis_index("rep")
    groups = lax.axis_size(ROW_COL)
    first_block = lax.axis_index(ROW_COL) * rows

    own = lax.dynamic_slice_in_dim(direction, rep * half, half, axis=1)
    one = lax.ppermute(own, ALL, halo_pairs(groups, 1))
    two = lax.ppermute(own, ALL, halo_pairs(groups, -1))
    other_gain = lax.ppermute(gain, "rep", [(0, 1), (1, 0)])
    res = lax.dynamic_slice_in_dim(residual, rep * half, half, axis=1)

    low = jnp.where(rep == 0, one, two)
    high = jnp.where(rep == 0, two, one)
    segments = jnp.concatenate([low, own, high], axis=0).reshape(rows + 2 * REACH, BLK, half)
    slots = gain.shape[1]
    mine = lax.dynamic_slice_in_dim(coupled_columns, rep * slots, slots, axis=1)
    theirs = lax.dynamic_slice_in_dim(coupled_columns, (1 - rep) * slots, slots, axis=1)
    shift = REACH - first_block
    image = jnp.einsum(
        "rkab,rkbs->ras",
        jnp.concatenate([gain, other_gain], axis=1),
        segments[jnp.concatenate([mine, theirs], axis=1) + shift],
        precision=lax.Precision.HIGHEST,
        preferred_element_type=jnp.float32,
    ).reshape(rows * BLK, half)
    other_image = lax.ppermute(image, "rep", [(0, 1), (1, 0)])

    sums = jnp.stack(
        [
            jnp.sum(res * res, axis=0),
            jnp.sum(own * image, axis=0),
            jnp.sum(res * image, axis=0),
            jnp.sum(image * image, axis=0),
        ]
    ).reshape(8, -1)
    n1 = lax.axis_size("row") * lax.axis_size("col_1")
    sums = jnp.sum(from_all(sums, ("row", "col_1"), n1).reshape(n1, *sums.shape), axis=0)
    n2 = lax.axis_size("col_0")
    sums = jnp.sum(from_all(sums, ("col_0", "rep"), 2 * n2).reshape(n2, 2, *sums.shape), axis=0)
    sums = jnp.concatenate([sums[0].reshape(4, half), sums[1].reshape(4, half)], axis=1)
    norm_old, curvature, crossing, image_square = sums

    left = jnp.where(rep == 0, image, other_image)
    right = jnp.where(rep == 0, other_image, image)
    image = jnp.concatenate([left, right], axis=1)
    step_size = norm_old / curvature
    solution_next = solution + step_size * direction
    residual_next = residual - step_size * image
    norm_new = norm_old - 2.0 * step_size * crossing + step_size * step_size * image_square
    direction_next = residual_next + norm_new / norm_old * direction
    return (solution_next, residual_next, direction_next)


def solution(mesh):
    finer = Mesh(
        mesh.devices.reshape(mesh.shape["row"], 8, 4, mesh.shape["rep"]),
        ALL,
    )
    return jax.shard_map(
        per_device,
        mesh=finer,
        in_specs=(
            P(ROW_COL, "rep", None, None),
            P(ROW_COL, None),
            P(ROW_COL, None),
            P(ROW_COL, None),
            P(ROW_COL, None),
        ),
        out_specs=(P(ROW_COL, None), P(ROW_COL, None), P(ROW_COL, None)),
        check_vma=False,
    )
```

time: 93 us -> 71 us (0.76)
  the two profiles are of different devices: /device:TPU:8 before, /device:TPU:1 now
where the time goes in v1:
time: 71 us; the launch traced here: 70.7 us
  blocking collectives  39.2 us (55%)
  starting transfers between devices  18.8 us (26%)
  local copies, waits for them, and re-layouts  4.45 us (6%)
  matrix products  3.97 us (6%)
  other arithmetic  2.16 us (3%)
  waiting for transfers between devices  1.34 us (2%)
  between operations  0.8 us (1%)
    all_to_all x2, blocking collectives, from_all(): lax.all_to_all(jnp.broadcast_to(x[None], (count, *x.shape)), axes, 0, 0,...  39.2 us
    ppermute x1, starting transfers between devices, per_device(): other_image = lax.ppermute(image, 'rep', [(0, 1), (1, 0)])  7.46 us
    ppermute x1, starting transfers between devices, per_device(): other_gain = lax.ppermute(gain, 'rep', [(0, 1), (1, 0)])  5.48 us
    ppermute x1, starting transfers between devices, per_device(): two = lax.ppermute(own, ALL, halo_pairs(groups, -1))  4.59 us
    dot_general x1, matrix products, per_device(): jnp.einsum('rkab,rkbs->ras', jnp.concatenate([gain, other_gain], axis=1),...  3.97 us
    gather x1, local copies, waits for them, and re-layouts, per_device(): segments[jnp.concatenate([mine, theirs], axis=1) + shift]  2.42 us
    add x1, other arithmetic, per_device(): direction_next = residual_next + norm_new / norm_old * direction  1.67 us
  transfers between devices with their start and end apart: 4, of which 1 were waited for; matrix products, arithmetic and copies ran while one was open for 5% of the time, Pallas kernels for 0%

profile of v1, /device:TPU:1, one launch (start us, length us, event | category | flops | bytes accessed | tf_op | source)
XLA Modules:
  0.0 70.7 jit_solution(17021460448588714516)
XLA Ops:
  0.6 1.0 %constant_dynamic-slice_fusion = f32[384,256]{1,0:T(8,128)S(1)} fusion(f32[384,512]{1,0:T(8,128)} %param.9, s32[]{:T(128)S(6)} %select_n.40), kind=kLoop, calls=%fused_computation.33 | loop fusion | bytes 786436 | tf_op jit(solution)/shard_map/dynamic_slice | solution.py:34
  1.7 1.3 %collective-permute-start.1 = (f32[384,256]{1,0:T(8,128)S(1)}, f32[384,256]{1,0:T(8,128)S(1)}, u32[]{:S(2)}, u32[]{:S(2)}) collective-permute-start(f32[384,256]{1,0:T(8,128)S(1)} %constant_dynamic-slice_fusion), channel_id=1, source_target_pairs={{0,2},{2,4},{3,1},{4,6},{5,3},{6,8},{7,5},{8,10},{9,7},{10,12},{11... | collective-permute-start | bytes 1179656 | tf_op jit(solution)/shard_map/ppermute | solution.py:35
  3.0 4.6 %collective-permute-start.2 = (f32[384,256]{1,0:T(8,128)S(1)}, f32[384,256]{1,0:T(8,128)S(1)}, u32[]{:S(2)}, u32[]{:S(2)}) collective-permute-start(f32[384,256]{1,0:T(8,128)S(1)} %constant_dynamic-slice_fusion), channel_id=1, source_target_pairs={{1,3},{2,0},{3,5},{4,2},{5,7},{6,4},{7,9},{8,6},{9,11},{10,8},{11,... | collective-permute-start | bytes 1179656 | tf_op jit(solution)/shard_map/ppermute | solution.py:36
  7.6 5.5 %collective-permute-start = (f32[3,4,128,128]{3,2,1,0:T(8,128)}, f32[3,4,128,128]{3,2,1,0:T(8,128)S(1)}, u32[]{:S(2)}, u32[]{:S(2)}) collective-permute-start(f32[3,4,128,128]{3,2,1,0:T(8,128)} %param.5), channel_id=1, source_target_pairs={{0,1},{1,0},{2,3},{3,2},{4,5},{5,4},{6,7},{7,6},{8,9},{9,8},{10,11... | collective-permute-start | bytes 2359304 | tf_op jit(solution)/shard_map/ppermute | solution.py:37
  13.0 0.8 %dynamic-slice_bitcast_fusion.1 = (s32[3,4,1]{1,0,2:T(4,128)S(1)}, s32[3,4,1]{1,0,2:T(4,128)S(1)}) fusion(s32[3,8]{1,0:T(4,128)} %param.6, s32[]{:T(128)S(6)} %select_n.44, s32[]{:T(128)S(6)} %select_n.45), kind=kLoop, calls=%fused_computation.32 | loop fusion | bytes 200 | tf_op jit(solution)/shard_map/concatenate | solution.py:50
  13.9 0.1 compare_select_fusion
  14.0 0.1 reshape.60
  14.1 0.0 collective-permute-done.1
  14.1 0.0 collective-permute-done.2
  14.1 0.1 broadcast_select_fusion.3
  14.1 0.1 pad_maximum_fusion
  14.2 0.0 copy-start.3
  14.2 2.4 %gather_fusion = f32[24,128,256]{2,1,0:T(8,128)} fusion(f32[9,128,256]{2,1,0:T(8,128)S(1)} %bitcast.27, s32[1024]{0:T(1024)S(1)} %pad_clamp_fusion), kind=kCustom, calls=%fused_computation | custom fusion | bytes 6291552 | tf_op jit(solution)/shard_map/gather | solution.py:50
  16.7 0.0 collective-permute-done
  16.7 0.0 copy-start.1
  16.7 4.0 %fusion.5 = (f32[256]{0:T(256)S(1)}, f32[3,128,256,1]{2,1,3,0:T(8,128)S(1)}) fusion(f32[3,8,128,256]{3,2,1,0:T(8,128)} %bitcast.28, f32[3,4,128,128]{3,2,1,0:T(8,128)S(1)} %collective-permute-done, f32[3,4,128,128]{3,2,1,0:T(8,128)S(1)} %copy-done.3), kind=kOutput, calls=%fused_computation.11 | convolution fusion | flops 1208549120 | bytes 5112832 | tf_op jit(solution)/shard_map/rkab,rkbs->ras/dot_general | solution.py:47
  20.6 0.0 copy-start.2
  20.7 7.5 %collective-permute-start.3 = (f32[384,256]{1,0:T(8,128)S(1)}, f32[384,256]{1,0:T(8,128)S(1)}, u32[]{:S(2)}, u32[]{:S(2)}) collective-permute-start(f32[384,256]{1,0:T(8,128)S(1)} %bitcast.29), channel_id=1, source_target_pairs={{0,1},{1,0},{2,3},{3,2},{4,5},{5,4},{6,7},{7,6},{8,9},{9,8},{10,11... | collective-permute-start | bytes 1179656 | tf_op jit(solution)/shard_map/ppermute | solution.py:54
  28.1 1.3 %collective-permute-done.3 = f32[384,256]{1,0:T(8,128)S(1)} collective-permute-done((f32[384,256]{1,0:T(8,128)S(1)}, f32[384,256]{1,0:T(8,128)S(1)}, u32[]{:S(2)}, u32[]{:S(2)}) %collective-permute-start.3) | collective-permute-done | bytes 393248 | tf_op jit(solution)/shard_map/ppermute | solution.py:54
  29.5 0.2 broadcast_select_fusion.1
  29.7 26.9 %all_to_all.10 = f32[32,8,128]{2,1,0:T(8,128)S(1)} all-to-all(f32[32,8,128]{2,1,0:T(8,128)S(1)} %broadcast_in_dim.7), channel_id=1, replica_groups=mesh['row'=8,'col_0'=8,'col_1'=4,'rep'=2] {'row','col_1'}, dimensions={0} | all-to-all | bytes 262144 | tf_op jit(solution)/shard_map/all_to_all | solution.py:23
  56.7 12.2 %all_to_all.11 = f32[16,8,128]{2,1,0:T(8,128)S(1)} all-to-all(f32[16,8,128]{2,1,0:T(8,128)S(1)} %broadcast_in_dim.8), channel_id=1, replica_groups=mesh['row'=8,'col_0'=8,'col_1'=4,'rep'=2] {'col_0','rep'}, dimensions={0} | all-to-all | bytes 131072 | tf_op jit(solution)/shard_map/all_to_all | solution.py:23
  69.0 0.0 copy-done.2
  69.0 1.7 %multiply_add_fusion = (f32[384,512]{1,0:T(8,128)}, f32[384,512]{1,0:T(8,128)}, f32[384,512]{1,0:T(8,128)}) fusion(f32[384,512]{1,0:T(8,128)S(1)} %copy-done, f32[512]{0:T(512)S(1)} %bitcast.31, f32[384,512]{1,0:T(8,128)S(1)} %copy-done.1, f32[384,256]{1,0:T(8,128)S(1)} %get-tuple-element.12, f32[384,256]{1,0:T(8,128)S(1)} %get-tuple-element.11, ...), kind=kLoop, calls=%fused_computation.8 | loop fusion | flops 1376256 | bytes 5509120 | tf_op jit(solution)/shard_map/add | solution.py:78
  (17 shorter events, 0.2 us)
Async XLA Ops:
  1.7 12.4 %collective-permute-start.1 = (f32[384,256]{1,0:T(8,128)S(1)}, f32[384,256]{1,0:T(8,128)S(1)}, u32[]{:S(2)}, u32[]{:S(2)}) collective-permute-start(f32[384,256]{1,0:T(8,128)S(1)} %constant_dynamic-slice_fusion), channel_id=1, source_target_pairs={{0,2},{2,4},{3,1},{4,6},{5,3},{6,8},{7,5},{8,10},{9,7},{10,12},{11... | collective-permute-start | bytes 1179656 | tf_op jit(solution)/shard_map/ppermute | solution.py:35
  3.0 11.1 %collective-permute-start.2 = (f32[384,256]{1,0:T(8,128)S(1)}, f32[384,256]{1,0:T(8,128)S(1)}, u32[]{:S(2)}, u32[]{:S(2)}) collective-permute-start(f32[384,256]{1,0:T(8,128)S(1)} %constant_dynamic-slice_fusion), channel_id=1, source_target_pairs={{1,3},{2,0},{3,5},{4,2},{5,7},{6,4},{7,9},{8,6},{9,11},{10,8},{11,... | collective-permute-start | bytes 1179656 | tf_op jit(solution)/shard_map/ppermute | solution.py:36
  7.6 9.1 %collective-permute-start = (f32[3,4,128,128]{3,2,1,0:T(8,128)}, f32[3,4,128,128]{3,2,1,0:T(8,128)S(1)}, u32[]{:S(2)}, u32[]{:S(2)}) collective-permute-start(f32[3,4,128,128]{3,2,1,0:T(8,128)} %param.5), channel_id=1, source_target_pairs={{0,1},{1,0},{2,3},{3,2},{4,5},{5,4},{6,7},{7,6},{8,9},{9,8},{10,11... | collective-permute-start | bytes 2359304 | tf_op jit(solution)/shard_map/ppermute | solution.py:37
  14.2 2.4 %copy-start.3 = (f32[3,4,128,128]{3,2,1,0:T(8,128)S(1)}, f32[3,4,128,128]{3,2,1,0:T(8,128)}, u32[]{:S(2)}) copy-start(f32[3,4,128,128]{3,2,1,0:T(8,128)} %param.5) | copy-start | bytes 2359300
  16.7 12.8 %copy-start = (f32[384,512]{1,0:T(8,128)S(1)}, f32[384,512]{1,0:T(8,128)}, u32[]{:S(2)}) copy-start(f32[384,512]{1,0:T(8,128)} %param.9) | copy-start | bytes 2359300
  16.7 12.8 %copy-start.1 = (f32[384,512]{1,0:T(8,128)S(1)}, f32[384,512]{1,0:T(8,128)}, u32[]{:S(2)}) copy-start(f32[384,512]{1,0:T(8,128)} %param.8) | copy-start | bytes 2359300
  20.6 48.4 %copy-start.2 = (f32[384,512]{1,0:T(8,128)S(1)}, f32[384,512]{1,0:T(8,128)}, u32[]{:S(2)}) copy-start(f32[384,512]{1,0:T(8,128)} %param.7) | copy-start | bytes 2359300
  20.7 8.8 %collective-permute-start.3 = (f32[384,256]{1,0:T(8,128)S(1)}, f32[384,256]{1,0:T(8,128)S(1)}, u32[]{:S(2)}, u32[]{:S(2)}) collective-permute-start(f32[384,256]{1,0:T(8,128)S(1)} %bitcast.29), channel_id=1, source_target_pairs={{0,1},{1,0},{2,3},{3,2},{4,5},{5,4},{6,7},{7,6},{8,9},{9,8},{10,11... | collective-permute-start | bytes 1179656 | tf_op jit(solution)/shard_map/ppermute | solution.py:54

commit v2 on v1

v2 whole, which is shorter than its diff:
```python
import jax
import jax.numpy as jnp
from jax import lax
from jax.experimental import pallas as pl
from jax.experimental.pallas import tpu as pltpu
from jax.sharding import Mesh
from jax.sharding import PartitionSpec as P

BLK = 128
REACH = 3
CHUNKS = 4
ROW_COL = ("row", "col_0", "col_1")
ALL = ("row", "col_0", "col_1", "rep")
F32, BF16 = jnp.float32, jnp.bfloat16


def halo_pairs(groups, first):
    pairs = []
    for rep in range(2):
        for p in range((rep + 1 - first) % 2, groups - 1, 2):
            near, far = 2 * p + rep, 2 * (p + 1) + rep
            pairs += [(near, far), (far, near)]
    return pairs


def split(x):
    top = x.astype(BF16)
    return top, (x - top.astype(F32)).astype(BF16)


def dot3(a_top, a_rest, x):
    x_top, x_rest = split(x)
    dot = lambda a, b: jnp.dot(a, b, preferred_element_type=F32)
    return dot(a_top, x_top) + (dot(a_top, x_rest) + dot(a_rest, x_top))


def place_blocks(columns, blocks, offset, dense):
    rows, slots = blocks.shape[0], blocks.shape[1]
    segment = lax.axis_index(ROW_COL)
    low_first = (segment + lax.axis_index("rep")) % 2 == 1
    for i in range(rows):
        for k in range(slots):
            w = columns[i, offset + k] - segment * rows + REACH
            low = jnp.where(low_first, w, w + 3)
            high = jnp.where(low_first, w - 3, w - 6)
            c = jnp.where(w < 3, low, jnp.where(w > 5, high, w + 3))
            here = pl.ds(i * BLK, BLK)
            dense[c, here, :] = dense[c, here, :] + blocks[i, k]


def begin(columns, gain, residual, direction, solution, dense, norm):
    rep = lax.axis_index("rep")
    half = residual.shape[1] // 2
    dense[...] = jnp.zeros_like(dense)
    place_blocks(columns, gain, rep * gain.shape[1], dense)
    r = residual[:, pl.ds(pl.multiple_of(rep * half, half), half)]
    norm[...] = jnp.sum(r * r, axis=0, keepdims=True)


def prepare(columns, other, own, start, top, rest, local, dense):
    dense[...] = start[...]
    place_blocks(columns, other, (1 - lax.axis_index("rep")) * other.shape[1], dense)
    for c in range(6):
        top[c], rest[c] = split(dense[c])
    middle = jnp.concatenate([dense[6], dense[7], dense[8]], axis=1)
    m_top, m_rest = split(middle)
    local[...] = dot3(m_top, m_rest, own[...])


def finish(one, two, top, rest, local, own, res, norm, image, sums):
    x = jnp.concatenate([one[...], two[...]], axis=0)
    product = local[...]
    half = product.shape[1]
    for pair in range(3):
        a_top = jnp.concatenate([top[2 * pair], top[2 * pair + 1]], axis=1)
        a_rest = jnp.concatenate([rest[2 * pair], rest[2 * pair + 1]], axis=1)
        product += dot3(a_top, a_rest, x[2 * pair * BLK : 2 * (pair + 1) * BLK])
    image[...] = product
    r = res[:, pl.ds(pl.multiple_of(lax.axis_index("rep") * half, half), half)]
    rows = [
        norm[...],
        jnp.sum(own[...] * product, axis=0, keepdims=True),
        jnp.sum(r * product, axis=0, keepdims=True),
        jnp.sum(product * product, axis=0, keepdims=True),
    ]
    packed = jnp.concatenate([v[:, h : h + BLK] for v in rows for h in range(0, half, BLK)], axis=0)
    sums[...] = jnp.broadcast_to(packed[None], sums.shape)


def fold(terms, sums):
    sums[...] = jnp.broadcast_to(jnp.sum(terms[...], axis=0)[None], sums.shape)


def update(terms, image, other, solution, residual, direction, sol_next, res_next, dir_next):
    half = image.shape[1]
    chunk = sol_next.shape[0]
    rep = lax.axis_index("rep")
    here = pl.ds(pl.multiple_of(pl.program_id(0) * chunk, chunk), chunk)
    for side in range(2):
        total = terms[side]
        for n in range(1, terms.shape[0] // 2):
            total += terms[2 * n + side]
        mine = rep == side
        for h in range(half // BLK):
            lanes = slice(side * half + h * BLK, side * half + (h + 1) * BLK)
            part = slice(h * BLK, (h + 1) * BLK)
            norm_old, curvature, crossing, square = (total[2 * n + h : 2 * n + h + 1] for n in range(4))
            step = norm_old / curvature
            norm_new = norm_old - 2.0 * step * crossing + step * step * square
            ratio = norm_new / norm_old
            product = jnp.where(mine, image[here, part], other[here, part])
            d = direction[here, lanes]
            sol_next[:, lanes] = solution[here, lanes] + step * d
            r = residual[here, lanes] - step * product
            res_next[:, lanes] = r
            dir_next[:, lanes] = r + ratio * d


def vmem(n):
    return [pl.BlockSpec(memory_space=pltpu.VMEM)] * n


def from_all(x, axes):
    return lax.all_to_all(x, axes, 0, 0, tiled=True)


def iteration(gain, coupled_columns, solution, residual, direction):
    rows, _ = gain.shape[:2]
    states, snapshots = direction.shape
    half = snapshots // 2
    rep = lax.axis_index("rep")
    groups = lax.axis_size(ROW_COL)

    own = lax.dynamic_slice_in_dim(direction, rep * half, half, axis=1)
    one = lax.ppermute(own, ALL, halo_pairs(groups, True))
    two = lax.ppermute(own, ALL, halo_pairs(groups, False))
    other_gain = lax.ppermute(gain, "rep", [(0, 1), (1, 0)])
    smem = pl.BlockSpec(memory_space=pltpu.SMEM)
    halves = jax.ShapeDtypeStruct((states, half), F32)
    whole = jax.ShapeDtypeStruct((states, snapshots), F32)
    terms = jax.ShapeDtypeStruct((2 * rows, states, BLK), BF16)
    band = jax.ShapeDtypeStruct((3 * rows, states, BLK), F32)
    dense, norm = pl.pallas_call(
        begin,
        out_shape=(band, jax.ShapeDtypeStruct((1, half), F32)),
        in_specs=[smem, *vmem(4)],
        out_specs=tuple(vmem(2)),
        cost_estimate=pl.CostEstimate(flops=4_000_000, bytes_accessed=5_000_000, transcendentals=0),
        compiler_params=pltpu.CompilerParams(vmem_limit_bytes=10 << 20),
        name="begin",
    )(coupled_columns, gain, residual, direction, solution)
    top, rest, local = pl.pallas_call(
        prepare,
        out_shape=(terms, terms, halves),
        in_specs=[smem, *vmem(3)],
        out_specs=tuple(vmem(3)),
        scratch_shapes=[pltpu.VMEM(band.shape, F32)],
        cost_estimate=pl.CostEstimate(flops=400_000_000, bytes_accessed=5_000_000, transcendentals=0),
        compiler_params=pltpu.CompilerParams(vmem_limit_bytes=10 << 20),
        name="prepare",
    )(coupled_columns, other_gain, own, dense)

    n1 = lax.axis_size("row") * lax.axis_size("col_1")
    n2 = 2 * lax.axis_size("col_0")
    image, sums = pl.pallas_call(
        finish,
        out_shape=(halves, jax.ShapeDtypeStruct((n1, 8, BLK), F32)),
        in_specs=vmem(8),
        out_specs=tuple(vmem(2)),
        cost_estimate=pl.CostEstimate(flops=500_000_000, bytes_accessed=5_000_000, transcendentals=0),
        compiler_params=pltpu.CompilerParams(vmem_limit_bytes=10 << 20),
        name="finish",
    )(one, two, top, rest, local, own, residual, norm)
    sums = from_all(sums, ("row", "col_1"))
    sums = pl.pallas_call(
        fold,
        out_shape=jax.ShapeDtypeStruct((n2, 8, BLK), F32),
        in_specs=vmem(1),
        out_specs=vmem(1)[0],
        compiler_params=pltpu.CompilerParams(vmem_limit_bytes=2 << 20),
        name="fold",
    )(sums)
    image, sums = lax.optimization_barrier((image, sums))
    other_image = lax.ppermute(image, "rep", [(0, 1), (1, 0)])
    sums = from_all(sums, ("col_0", "rep"))

    chunk = states // CHUNKS
    block = pl.BlockSpec((chunk, snapshots), lambda c: (c, 0))
    return pl.pallas_call(
        update,
        grid=(CHUNKS,),
        out_shape=(whole, whole, whole),
        in_specs=vmem(6),
        out_specs=(block, block, block),
        compiler_params=pltpu.CompilerParams(vmem_limit_bytes=10 << 20),
        name="update",
    )(sums, image, other_image, solution, residual, direction)


def solution(mesh):
    finer = Mesh(
        mesh.devices.reshape(mesh.shape["row"], 8, 4, mesh.shape["rep"]),
        ALL,
    )
    return jax.shard_map(
        iteration,
        mesh=finer,
        in_specs=(
            P(ROW_COL, "rep", None, None),
            P(ROW_COL, None),
            P(ROW_COL, None),
            P(ROW_COL, None),
            P(ROW_COL, None),
        ),
        out_specs=(P(ROW_COL, None), P(ROW_COL, None), P(ROW_COL, None)),
        check_vma=False,
    )
```

time: 71 us -> 65.8 us (0.927)
  Pallas kernels: 0 us -> 4.94 us
  starting transfers between devices: 18.8 us -> 14.7 us
  matrix products: 3.97 us -> 0 us
  blocking collectives: 39.2 us -> 35.6 us
  other arithmetic: 2.16 us -> 0 us
  waiting for transfers between devices: 1.34 us -> 3.14 us
  local copies, waits for them, and re-layouts: 4.45 us -> 6.25 us
    unnamed x9 -> x16, local copies, waits for them, and re-layouts: 0.03 us -> 5.22 us
    pallas_call x0 -> x5, Pallas kernels: none -> 4.94 us  [the longest x1 1.97 us: iteration(): pl.pallas_call(update, grid=(CHUNKS,), out_shape=(whole, whole, whole), i...]
    ppermute x4, starting transfers between devices: 18.8 us -> 14.7 us  [the longest x1 8.75 us: iteration(): other_gain = lax.ppermute(gain, 'rep', [(0, 1), (1, 0)])]
    dot_general x1 -> x0, matrix products: 3.97 us -> none  [per_device(): jnp.einsum('rkab,rkbs->ras', jnp.concatenate([gain, other_gain], axis=1),...]
    all_to_all x2, blocking collectives: 39.2 us -> 35.6 us  [from_all(): return lax.all_to_all(x, axes, 0, 0, tiled=True)]
    gather x1 -> x0, local copies, waits for them, and re-layouts: 2.42 us -> none  [per_device(): segments[jnp.concatenate([mine, theirs], axis=1) + shift]]
    ppermute x4, waiting for transfers between devices: 1.34 us -> 3.14 us  [the longest x1 3.13 us: iteration(): two = lax.ppermute(own, ALL, halo_pairs(groups, False))]
    add x1 -> x0, other arithmetic: 1.67 us -> none  [per_device(): direction_next = residual_next + norm_new / norm_old * direction]
  transfers between devices with their start and end apart: 4 -> 4, of which waited for: 1 -> 1; matrix products, arithmetic and copies ran while one was open for 5% -> 2% of each run, Pallas kernels for 0% -> 3%
where the time goes in v2:
time: 65.8 us; the launch traced here: 65.3 us
  blocking collectives  35.6 us (54%)
  starting transfers between devices  14.7 us (22%)
  local copies, waits for them, and re-layouts  6.25 us (9%)
  Pallas kernels  4.94 us (8%)
  waiting for transfers between devices  3.14 us (5%)
  between operations  0.73 us (1%)
    all_to_all x2, blocking collectives, from_all(): return lax.all_to_all(x, axes, 0, 0, tiled=True)  35.6 us
    ppermute x1, starting transfers between devices, iteration(): other_gain = lax.ppermute(gain, 'rep', [(0, 1), (1, 0)])  8.75 us
    unnamed x16, local copies, waits for them, and re-layouts  5.22 us
    ppermute x1, starting transfers between devices, iteration(): other_image = lax.ppermute(image, 'rep', [(0, 1), (1, 0)])  3.35 us
    ppermute x1, waiting for transfers between devices, iteration(): two = lax.ppermute(own, ALL, halo_pairs(groups, False))  3.13 us
    pallas_call x1, Pallas kernels, iteration(): pl.pallas_call(update, grid=(CHUNKS,), out_shape=(whole, whole, whole), i...  1.97 us
    ppermute x1, starting transfers between devices, iteration(): two = lax.ppermute(own, ALL, halo_pairs(groups, False))  1.92 us
    pallas_call x1, Pallas kernels, iteration(): pl.pallas_call(prepare, out_shape=(terms, terms, halves), in_specs=[smem,...  1.45 us
  transfers between devices with their start and end apart: 4, of which 1 were waited for; matrix products, arithmetic and copies ran while one was open for 2% of the time, Pallas kernels for 3%

profile of v2, /device:TPU:1, one launch (start us, length us, event | category | flops | bytes accessed | tf_op | source)
XLA Modules:
  0.0 65.3 jit_solution(11465165541937715871)
XLA Ops:
  0.6 8.7 %collective-permute-start.2 = (f32[3,4,128,128]{3,2,1,0:T(8,128)}, f32[3,4,128,128]{3,2,1,0:T(8,128)S(1)}, u32[]{:S(2)}, u32[]{:S(2)}) collective-permute-start(f32[3,4,128,128]{3,2,1,0:T(8,128)} %gain.1), channel_id=1, source_target_pairs={{0,1},{1,0},{2,3},{3,2},{4,5},{5,4},{6,7},{7,6},{8,9},{9,8},{10,11... | collective-permute-start | bytes 2359304 | tf_op jit(solution)/shard_map/ppermute | solution.py:137
  9.4 1.0 %constant_dynamic-slice_fusion.own = f32[384,256]{1,0:T(8,128)S(1)} fusion(f32[384,512]{1,0:T(8,128)} %direction.3, s32[]{:T(128)S(6)} %select_n.3), kind=kLoop, calls=%fused_computation | loop fusion | bytes 786436 | tf_op jit(solution)/shard_map/dynamic_slice | solution.py:134
  10.4 0.7 %collective-permute-start = (f32[384,256]{1,0:T(8,128)S(1)}, f32[384,256]{1,0:T(8,128)S(1)}, u32[]{:S(2)}, u32[]{:S(2)}) collective-permute-start(f32[384,256]{1,0:T(8,128)S(1)} %constant_dynamic-slice_fusion.own), channel_id=1, source_target_pairs={{0,2},{2,0},{4,6},{6,4},{8,10},{10,8},{12,14},{14,12},{16,18},{18,... | collective-permute-start | bytes 1179656 | tf_op jit(solution)/shard_map/ppermute | solution.py:135
  11.1 1.9 %collective-permute-start.1 = (f32[384,256]{1,0:T(8,128)S(1)}, f32[384,256]{1,0:T(8,128)S(1)}, u32[]{:S(2)}, u32[]{:S(2)}) collective-permute-start(f32[384,256]{1,0:T(8,128)S(1)} %constant_dynamic-slice_fusion.own), channel_id=1, source_target_pairs={{2,4},{4,2},{6,8},{8,6},{10,12},{12,10},{14,16},{16,14},{18,20},{2... | collective-permute-start | bytes 1179656 | tf_op jit(solution)/shard_map/ppermute | solution.py:136
  13.0 0.0 copy-start
  13.1 1.1 %copy-done = f32[384,512]{1,0:T(8,128)S(1)} copy-done((f32[384,512]{1,0:T(8,128)S(1)}, f32[384,512]{1,0:T(8,128)}, u32[]{:S(2)}) %copy-start) | copy-done | bytes 786456
  14.2 1.1 %copy-done.2 = f32[384,512]{1,0:T(8,128)S(1)} copy-done((f32[384,512]{1,0:T(8,128)S(1)}, f32[384,512]{1,0:T(8,128)}, u32[]{:S(2)}) %copy-start.2) | copy-done | bytes 786456
  15.3 1.1 %copy-done.4 = f32[384,512]{1,0:T(8,128)S(1)} copy-done((f32[384,512]{1,0:T(8,128)S(1)}, f32[384,512]{1,0:T(8,128)}, u32[]{:S(2)}) %copy-start.4) | copy-done | bytes 786456
  16.4 1.1 %copy-done.6 = f32[3,4,128,128]{3,2,1,0:T(8,128)S(1)} copy-done((f32[3,4,128,128]{3,2,1,0:T(8,128)S(1)}, f32[3,4,128,128]{3,2,1,0:T(8,128)}, u32[]{:S(2)}) %copy-start.6) | copy-done | bytes 786456
  17.6 0.7 %copy-done.7 = s32[3,8]{1,0:T(4,128)S(1)} copy-done((s32[3,8]{1,0:T(4,128)S(1)}, s32[3,8]{1,0:T(4,128)}, u32[]{:S(2)}) %copy-start.7) | copy-done | bytes 120
  18.3 0.8 %begin.1 = (f32[9,384,128]{2,1,0:T(8,128)S(1)}, f32[1,256]{1,0:T(1,128)S(1)}) custom-call(s32[3,8]{1,0:T(4,128)S(1)} %copy-done.7, f32[3,4,128,128]{3,2,1,0:T(8,128)S(1)} %copy-done.6, f32[384,512]{1,0:T(8,128)S(1)} %copy-done, f32[384,512]{1,0:T(8,128)S(1)} %copy-done.2, f32[384,512]{1,0:T(8,128)S(1)} %copy-done.4), custom_call_target="tpu_custom_call" | custom-call | flops 4000000 | bytes 5000000 | tf_op jit(solution)/shard_map/begin/pallas_call | solution.py:143
  19.1 0.0 copy-start.1
  19.1 0.0 collective-permute-done.2.other
  19.1 1.4 %prepare.1 = (bf16[6,384,128]{2,1,0:T(8,128)(2,1)S(1)}, bf16[6,384,128]{2,1,0:T(8,128)(2,1)S(1)}, f32[384,256]{1,0:T(8,128)S(1)}) custom-call(s32[3,8]{1,0:T(4,128)S(1)} %copy-done.7, f32[3,4,128,128]{3,2,1,0:T(8,128)S(1)} %collective-permute-done.2.other, f32[384,256]{1,0:T(8,128)S(1)} %constant_dynamic-slice_fusion.own, ...), custom_call_target="tpu_custom_call" | custom-call | flops 400000000 | bytes 5000000 | tf_op jit(solution)/shard_map/prepare/pallas_call | solution.py:152
  20.6 0.0 collective-permute-done.one
  20.6 3.1 %collective-permute-done.1.two = f32[384,256]{1,0:T(8,128)S(1)} collective-permute-done((f32[384,256]{1,0:T(8,128)S(1)}, f32[384,256]{1,0:T(8,128)S(1)}, u32[]{:S(2)}, u32[]{:S(2)}) %collective-permute-start.1) | collective-permute-done | bytes 393248 | tf_op jit(solution)/shard_map/ppermute | solution.py:136
  23.7 0.0 copy-done.1
  23.7 0.7 %finish.1 = (f32[384,256]{1,0:T(8,128)S(1)}, f32[32,8,128]{2,1,0:T(8,128)S(1)}) custom-call(f32[384,256]{1,0:T(8,128)S(1)} %collective-permute-done.one, f32[384,256]{1,0:T(8,128)S(1)} %collective-permute-done.1.two, bf16[6,384,128]{2,1,0:T(8,128)(2,1)S(1)} %get-tuple-element.13.top, bf16[6,384,128]{2,1,0:T(8,128)(2,1)S(1)} %get-tuple-element.14.rest, ...), custom_call_target="tpu_custom_call" | custom-call | flops 500000000 | bytes 5000000 | tf_op jit(solution)/shard_map/finish/pallas_call | solution.py:165
  24.4 21.9 %all_to_all.10.terms = f32[32,8,128]{2,1,0:T(8,128)S(1)} all-to-all(f32[32,8,128]{2,1,0:T(8,128)S(1)} %get-tuple-element.18), channel_id=1, replica_groups=mesh['row'=8,'col_0'=8,'col_1'=4,'rep'=2] {'row','col_1'}, dimensions={0} | all-to-all | bytes 262144 | tf_op jit(solution)/shard_map/all_to_all | solution.py:124
  46.3 3.3 %collective-permute-start.3 = (f32[384,256]{1,0:T(8,128)S(1)}, f32[384,256]{1,0:T(8,128)S(1)}, u32[]{:S(2)}, u32[]{:S(2)}) collective-permute-start(f32[384,256]{1,0:T(8,128)S(1)} %get-tuple-element.20.image), channel_id=1, source_target_pairs={{0,1},{1,0},{2,3},{3,2},{4,5},{5,4},{6,7},{7,6},{8,9},{9,8},{10,11... | collective-permute-start | bytes 1179656 | tf_op jit(solution)/shard_map/ppermute | solution.py:184
  49.7 13.7 %all_to_all.11.terms = f32[16,8,128]{2,1,0:T(8,128)S(1)} all-to-all(f32[16,8,128]{2,1,0:T(8,128)S(1)} %fold.1), channel_id=1, replica_groups=mesh['row'=8,'col_0'=8,'col_1'=4,'rep'=2] {'col_0','rep'}, dimensions={0} | all-to-all | bytes 131072 | tf_op jit(solution)/shard_map/all_to_all | solution.py:124
  63.3 0.0 collective-permute-done.3.other
  63.3 0.0 copy-done.3
  63.3 2.0 %update.1 = (f32[384,512]{1,0:T(8,128)}, f32[384,512]{1,0:T(8,128)}, f32[384,512]{1,0:T(8,128)}) custom-call(f32[16,8,128]{2,1,0:T(8,128)S(1)} %all_to_all.11.terms, f32[384,256]{1,0:T(8,128)S(1)} %get-tuple-element.20.image, f32[384,256]{1,0:T(8,128)S(1)} %collective-permute-done.3.other, f32[384,512]{1,0:T(8,128)S(1)} %copy-done.5, ...), custom_call_target="tpu_custom_call" | custom-call | tf_op jit(solution)/shard_map/update/pallas_call | solution.py:189
  (8 shorter events, 0.0 us)
Async XLA Ops:
  0.6 18.5 %collective-permute-start.2 = (f32[3,4,128,128]{3,2,1,0:T(8,128)}, f32[3,4,128,128]{3,2,1,0:T(8,128)S(1)}, u32[]{:S(2)}, u32[]{:S(2)}) collective-permute-start(f32[3,4,128,128]{3,2,1,0:T(8,128)} %gain.1), channel_id=1, source_target_pairs={{0,1},{1,0},{2,3},{3,2},{4,5},{5,4},{6,7},{7,6},{8,9},{9,8},{10,11... | collective-permute-start | bytes 2359304 | tf_op jit(solution)/shard_map/ppermute | solution.py:137
  10.4 10.1 %collective-permute-start = (f32[384,256]{1,0:T(8,128)S(1)}, f32[384,256]{1,0:T(8,128)S(1)}, u32[]{:S(2)}, u32[]{:S(2)}) collective-permute-start(f32[384,256]{1,0:T(8,128)S(1)} %constant_dynamic-slice_fusion.own), channel_id=1, source_target_pairs={{0,2},{2,0},{4,6},{6,4},{8,10},{10,8},{12,14},{14,12},{16,18},{18,... | collective-permute-start | bytes 1179656 | tf_op jit(solution)/shard_map/ppermute | solution.py:135
  11.1 12.6 %collective-permute-start.1 = (f32[384,256]{1,0:T(8,128)S(1)}, f32[384,256]{1,0:T(8,128)S(1)}, u32[]{:S(2)}, u32[]{:S(2)}) collective-permute-start(f32[384,256]{1,0:T(8,128)S(1)} %constant_dynamic-slice_fusion.own), channel_id=1, source_target_pairs={{2,4},{4,2},{6,8},{8,6},{10,12},{12,10},{14,16},{16,14},{18,20},{2... | collective-permute-start | bytes 1179656 | tf_op jit(solution)/shard_map/ppermute | solution.py:136
  13.0 1.1 %copy-start = (f32[384,512]{1,0:T(8,128)S(1)}, f32[384,512]{1,0:T(8,128)}, u32[]{:S(2)}) copy-start(f32[384,512]{1,0:T(8,128)} %residual.3) | copy-start | bytes 2359300
  14.2 1.1 %copy-start.2 = (f32[384,512]{1,0:T(8,128)S(1)}, f32[384,512]{1,0:T(8,128)}, u32[]{:S(2)}) copy-start(f32[384,512]{1,0:T(8,128)} %direction.3) | copy-start | bytes 2359300
  15.3 1.1 %copy-start.4 = (f32[384,512]{1,0:T(8,128)S(1)}, f32[384,512]{1,0:T(8,128)}, u32[]{:S(2)}) copy-start(f32[384,512]{1,0:T(8,128)} %solution.3) | copy-start | bytes 2359300
  16.4 1.1 %copy-start.6 = (f32[3,4,128,128]{3,2,1,0:T(8,128)S(1)}, f32[3,4,128,128]{3,2,1,0:T(8,128)}, u32[]{:S(2)}) copy-start(f32[3,4,128,128]{3,2,1,0:T(8,128)} %gain.1) | copy-start | bytes 2359300
  17.6 0.7 %copy-start.7 = (s32[3,8]{1,0:T(4,128)S(1)}, s32[3,8]{1,0:T(4,128)}, u32[]{:S(2)}) copy-start(s32[3,8]{1,0:T(4,128)} %columns.3) | copy-start | bytes 292
  19.1 4.6 %copy-start.1 = (f32[384,512]{1,0:T(8,128)S(1)}, f32[384,512]{1,0:T(8,128)}, u32[]{:S(2)}) copy-start(f32[384,512]{1,0:T(8,128)} %residual.3) | copy-start | bytes 2359300
  23.7 39.6 %copy-start.3 = (f32[384,512]{1,0:T(8,128)S(1)}, f32[384,512]{1,0:T(8,128)}, u32[]{:S(2)}) copy-start(f32[384,512]{1,0:T(8,128)} %direction.3) | copy-start | bytes 2359300
  23.7 39.6 %copy-start.5 = (f32[384,512]{1,0:T(8,128)S(1)}, f32[384,512]{1,0:T(8,128)}, u32[]{:S(2)}) copy-start(f32[384,512]{1,0:T(8,128)} %solution.3) | copy-start | bytes 2359300
  46.3 17.0 %collective-permute-start.3 = (f32[384,256]{1,0:T(8,128)S(1)}, f32[384,256]{1,0:T(8,128)S(1)}, u32[]{:S(2)}, u32[]{:S(2)}) collective-permute-start(f32[384,256]{1,0:T(8,128)S(1)} %get-tuple-element.20.image), channel_id=1, source_target_pairs={{0,1},{1,0},{2,3},{3,2},{4,5},{5,4},{6,7},{7,6},{8,9},{9,8},{10,11... | collective-permute-start | bytes 1179656 | tf_op jit(solution)/shard_map/ppermute | solution.py:184
